TPU v7x, 256 devices: a whole 4x4x8 slice. The times are simulated.
256 devices in a mesh: row: 32 (over y, z), col: 8 (over x, core).
Axes of the slice: x: 4, y: 4, z: 8, core: 2. Of those that a mesh axis runs over, the one named last changes fastest.
Arguments:
- tile_u: bfloat16 [3, 32, 2, 8, 512, 128], P(None, 'row', None, 'col'), may hold values from -6 to 6
- tile_v: bfloat16 [3, 32, 2, 8, 512, 128], P(None, 'row', None, 'col'), may hold values from -6 to 6
- tile_ranks: int32 [3, 32, 2, 8], P(None, 'row', None, 'col'), may hold values from 16 to 128
- lower_inverse: bfloat16 [2, 512, 512], replicated, as said below
- upper_inverse: bfloat16 [2, 512, 512], replicated, as said below
- row_order: int32 [2, 512], replicated, may hold values from 0 to 511, each once within a row
- sketch: bfloat16 [512, 128], replicated, may hold values from -0.25 to 0.25
Outputs:
- new_u: bfloat16 [3, 32, 2, 8, 512, 128], P(None, 'row', None, 'col')
- new_v: bfloat16 [3, 32, 2, 8, 512, 128], P(None, 'row', None, 'col')
Inputs may be any that keep to these rules, and one draw needn't show every extreme that they name: Each row of row_order names every number of 0 to 511 once. Each lower_inverse[k] is lower triangular with a unit diagonal. Each upper_inverse[k] is upper triangular with a positive diagonal.
All inputs are finite; a program needn't handle non-finite values.
Results may differ from a plain program's by a relative error of at most 0.03.
Values may be sent and summed in bfloat16 or wider, within the bound.
No kernel may reach another device: no remote copies, remote signals or barrier semaphores. Data moves between devices by JAX's collectives and lax.ppermute only.
A program may use at most 64 MiB of HBM per device.

v0:
```python
import functools

import jax
import jax.numpy as jnp
from jax import lax
from jax.experimental import pallas as pl
from jax.experimental.pallas import tpu as pltpu
from jax.sharding import Mesh
from jax.sharding import PartitionSpec as P


PANELS = 2
STEP = 16
F32 = jnp.float32
BF16 = jnp.bfloat16


def dot_nn(a, b):
    return lax.dot_general(a, b, (((1,), (0,)), ((), ())), preferred_element_type=F32)


def dot_nt(a, b):
    return lax.dot_general(a, b, (((1,), (1,)), ((), ())), preferred_element_type=F32)


def dot_tn(a, b):
    return lax.dot_general(a, b, (((0,), (0,)), ((), ())), preferred_element_type=F32)


def halves(x):
    high = x.astype(BF16)
    return high, (x - high.astype(F32)).astype(BF16)


def thirds(x):
    high = x.astype(BF16)
    rest = x - high.astype(F32)
    middle = rest.astype(BF16)
    return high, middle, (rest - middle.astype(F32)).astype(BF16)


def factor_block(rows, blocks, start, lane, sub):
    count = len(rows) * 8
    cols = [
        [
            jnp.broadcast_to(blocks[h][:, c : c + 1], (8, 128))
            if c < 8 * (h + 1)
            else None
            for h in range(len(rows))
        ]
        for c in range(count)
    ]
    panel = []
    for h in range(len(rows)):
        own = (lane >= start) & (lane < start + count)
        unit = (lane == sub + (start + 8 * h)).astype(F32)
        panel.append(jnp.where(own, unit, rows[h]))
    done = [jnp.zeros((8, 128), F32) for _ in rows]
    for p in range(count):
        hp, sp = divmod(p, 8)
        pivot = jnp.broadcast_to(cols[p][hp][sp : sp + 1, :], (8, 128))
        scale = lax.rsqrt(pivot)
        line = jnp.broadcast_to(panel[hp][sp : sp + 1, :], (8, 128)) * scale
        done[hp] = jnp.where(sub == sp, line, done[hp])
        scaled = {}
        for h in range(hp, len(rows)):
            if h == hp:
                if sp == 7:
                    continue
                scaled[h] = jnp.where(sub > sp, cols[p][h] * scale, 0.0)
            else:
                scaled[h] = cols[p][h] * scale
        for h, f in scaled.items():
            panel[h] = panel[h] - f * line
        for c in range(p + 1, count):
            hc, sc = divmod(c, 8)
            head = jnp.broadcast_to(scaled[hc][sc : sc + 1, :], (8, 128))
            for h, f in scaled.items():
                if h >= hc:
                    cols[c][h] = cols[c][h] - f * head
    return done


def compress_kernel(panel_id, tiles, places, sends, grid, info, *refs):
    groups = 1 + max(g for g, _ in places.values())
    us, vs = refs[:groups], refs[groups : 2 * groups]
    parts = refs[2 * groups : 2 * groups + 4]
    (half, other, lp, upper, sketch) = refs[2 * groups + 4 : 2 * groups + 9]
    outs = refs[2 * groups + 9 : len(refs) - 10]
    (top, sk_t, turned, side, side_u, vl_t, nupd, sample, mat, inv) = refs[len(refs) - 10 :]
    row_place = info[0]
    col_place = info[1]
    n_row, n_col = grid
    first_core = info[8] == 0
    y = info[9]
    lefts = sorted({a for a, _ in tiles})
    tops = sorted({e for _, e in tiles})
    rank_width = sketch.shape[1]
    tile_size = sketch.shape[0]
    root_b = tile_size**0.5
    lane = lax.broadcasted_iota(jnp.int32, (8, 128), 1)
    sub = lax.broadcasted_iota(jnp.int32, (8, 128), 0)
    lane_row = lax.broadcasted_iota(jnp.int32, (1, 128), 1)

    def rank_of(a, e):
        return info[2 + a * 2 + e]

    def load(which, a, e):
        group, index = places[a, e]
        value = which[group][index]
        if panel_id == 0:
            value = value * (lane_row < rank_of(a, e)).astype(F32).astype(BF16)
        return value

    for k in range(4):
        turn = (k - y + 4) % 4
        near = jnp.where(turn == 0, parts[0][...], parts[1][...])
        far = jnp.where(turn == 2, parts[2][...], parts[3][...])
        if k % 2 in tops:
            top[k] = jnp.where(turn < 2, near, far)
    sk_t[...] = sketch[...].T
    for e in tops:
        turned[e] = dot_nn(lp[panel_id], top[e]).astype(BF16)
    upper_t = upper[panel_id].T
    for a in lefts:
        side_u[a] = jnp.where(first_core, half[a], other[a])
        raw_v = jnp.where(first_core, other[a], half[a])
        wide = (dot_nn(upper_t, raw_v) * root_b).astype(BF16)
        side[a] = wide
        vl_t[a] = wide.T
    probe_top = {e: dot_nn(sk_t[...], top[2 + e]) for e in tops}

    for t, (a, e) in enumerate(tiles):
        coupling = (dot_nn(vl_t[a], turned[e]) * (1.0 / root_b)).astype(BF16)
        product = dot_nn(side_u[a], coupling)
        nupd[t] = (product * (-(rank_width**-0.5))).astype(BF16)
        probe_own = dot_nn(sk_t[...], load(vs, a, e))
        high, low = halves(jnp.concatenate([probe_own, probe_top[e]], axis=1))
        both = dot_nt(
            jnp.concatenate([load(us, a, e), nupd[t]], axis=1),
            jnp.concatenate([high, low], axis=0),
        )
        drawn = both[:, :rank_width] + both[:, rank_width:]
        drawn = jnp.where(lane_row < rank_of(a, e), drawn, 0.0)
        high, low = halves(drawn)
        sample[t] = jnp.concatenate([high, low], axis=1)
        gram = dot_tn(sample[t], sample[t])
        w = rank_width
        cross = gram[:w, w:]
        gram = (gram[:w, :w] + gram[w:, w:]) + (cross + gram[w:, :w])
        diag = lax.broadcasted_iota(jnp.int32, (w, w), 0)
        cols = lax.broadcasted_iota(jnp.int32, (w, w), 1)
        mat[t] = gram + jnp.where((diag == cols) & (cols >= rank_of(a, e)), 1.0, 0.0)

    def update(scaled):
        h, m, l = thirds(scaled)
        first = jnp.concatenate([h, h, m, m, h, l], axis=0)
        return first.T, jnp.concatenate([h, m, h, m, l, h], axis=0)

    for start in range(0, rank_width, STEP):
        stop = start + STEP
        for t in range(len(tiles)):
            rows = [mat[t, start + 8 * h : start + 8 * h + 8, :] for h in range(STEP // 8)]
            blocks = [row[:, start:stop] for row in rows]
            done = factor_block(rows, blocks, start, lane, sub)
            for h, piece in enumerate(done):
                inv[t, start + 8 * h : start + 8 * h + 8, :] = jnp.where(
                    lane < stop, piece, 0.0
                )
            if stop < rank_width:
                first, second = update(jnp.concatenate(done, axis=0))
                change = dot_nn(first[stop:, :], second)
                own = (lane_row >= start) & (lane_row < stop)
                mat[t, stop:, :] = jnp.where(own, 0.0, mat[t, stop:, :]) - change

    for t, (a, e) in enumerate(tiles):
        high, low = halves(inv[t])
        weights = jnp.concatenate(
            [
                jnp.concatenate([high, high], axis=1),
                jnp.concatenate([low, jnp.zeros_like(low)], axis=1),
            ],
            axis=0,
        )
        both = dot_nt(sample[t], weights)
        basis = both[:, :rank_width] + both[:, rank_width:]
        fresh_u = (basis * root_b).astype(BF16)
        keep_u = load(us, a, e)
        keep_v = load(vs, a, e)
        mixed = dot_tn(fresh_u, jnp.concatenate([keep_u, nupd[t]], axis=1))
        own_right = jnp.concatenate([keep_v, top[2 + e]], axis=1)
        if panel_id == PANELS - 1:
            right = dot_nt(own_right, mixed.astype(BF16))
        else:
            both = dot_nt(own_right, jnp.concatenate(halves(mixed), axis=0))
            right = both[:, :rank_width] + both[:, rank_width:]
        fresh_v = (right * (1.0 / tile_size)).astype(BF16)
        row_id = a * n_row + row_place
        col_id = e * n_col + col_place
        chosen = (row_id > panel_id) & (col_id > panel_id)
        settled = a * n_row > panel_id and e * n_col > panel_id
        if a == 0:
            keep_u = jnp.where((row_place == panel_id) & (col_id > panel_id), turned[e], keep_u)
        if e == 0:
            keep_v = jnp.where((col_place == panel_id) & (row_id > panel_id), side[a], keep_v)
        new_u = fresh_u if settled else jnp.where(chosen, fresh_u, keep_u)
        new_v = fresh_v if settled else jnp.where(chosen, fresh_v, keep_v)
        for out, index in sends[a, e][0]:
            outs[out][index] = new_u
        for out, index in sends[a, e][1]:
            outs[out][index] = new_v


def compress(
    panel_id, tiles, places, sends, depths, info, us, vs, parts, *shared
):
    count = len(tiles)
    size, width = shared[-1].shape
    vmem = pl.BlockSpec(memory_space=pltpu.VMEM)
    grid = (lax.axis_size(ROW), lax.axis_size(COL))
    flops = 2 * count * size * width * width * 30
    return pl.pallas_call(
        functools.partial(compress_kernel, panel_id, tiles, places, sends, grid),
        out_shape=[
            jax.ShapeDtypeStruct((depth,) * (depth > 0) + (size, width), BF16) for depth in depths
        ],
        in_specs=[pl.BlockSpec(memory_space=pltpu.SMEM)] + [vmem] * (2 * len(us) + 9),
        out_specs=[vmem] * len(depths),
        scratch_shapes=[
            pltpu.VMEM((4, size, width), BF16),
            pltpu.VMEM((width, size), BF16),
            pltpu.VMEM((2, size, width), BF16),
            pltpu.VMEM((3, size, width), BF16),
            pltpu.VMEM((3, size, width), BF16),
            pltpu.VMEM((3, width, size), BF16),
            pltpu.VMEM((count, size, width), BF16),
            pltpu.VMEM((count, size, 2 * width), BF16),
            pltpu.VMEM((count, width, width), F32),
            pltpu.VMEM((count, width, width), F32),
        ],
        compiler_params=pltpu.CompilerParams(vmem_limit_bytes=10 * 2**20),
        cost_estimate=pl.CostEstimate(
            flops=flops, bytes_accessed=8 * count * size * width, transcendentals=0
        ),
    )(info, *us, *vs, *parts, *shared)


ROW = ("y", "z")
COL = ("x", "core")


def spread_row(pieces, root):
    n_y, n_z = lax.axis_size("y"), lax.axis_size("z")
    y, z = lax.axis_index("y"), lax.axis_index("z")
    part = jnp.where((y == 0) & (z == root), pieces[0], 0)
    sent = [lax.ppermute(pieces[k], ROW, [(root, k * n_z + root)]) for k in range(1, n_y)]
    part = part + sent[0] + sent[1] + sent[2]

    def along_z(hops):
        pairs = [
            (k * n_z + (root + a) % n_z, k * n_z + (root + b) % n_z)
            for k in range(n_y)
            for a, b in hops
        ]
        return lax.ppermute(part, ROW, pairs)

    sent = [along_z([(0, 3)]), along_z([(0, 5)])]
    part = part + sent[0] + sent[1]
    sent = [along_z([(0, 1), (3, 4), (5, 6)]), along_z([(0, 7), (3, 2)])]
    part = part + sent[0] + sent[1]
    sent = [lax.ppermute(part, "y", [((k + s) % n_y, k) for k in range(n_y)]) for s in (2, 1, 3)]
    return [part, sent[1], sent[0], sent[2]]


def spread_col(side_u, side_v, root):
    n_core = lax.axis_size("core")
    x, core = lax.axis_index("x"), lax.axis_index("core")
    kept, given = (side_u, side_v) if root == 0 else (side_v, side_u)
    sent = lax.ppermute(given, COL, [(root, n_core - 1 - root)])
    start = jnp.where(x == 0, jnp.where(core == root, kept, sent), 0)
    sent = [lax.ppermute(start, "x", [(0, 1)]), lax.ppermute(start, "x", [(0, 3)])]
    half = start + sent[0] + sent[1]
    cut = half.shape[1] // 2
    low = lax.ppermute(half[:, :cut], "x", [(1, 2)])
    high = lax.ppermute(half[:, cut:], "x", [(3, 2)])
    half = half + jnp.concatenate([low, high], axis=1)
    other = lax.ppermute(half, "core", [(0, 1), (1, 0)])
    return half, other


ALL = ((0, 0), (0, 1), (1, 0), (1, 1), (2, 0), (2, 1))
HEAD = ((0, 0), (0, 1), (1, 0), (2, 0))
INNER = ((1, 1), (2, 1))
WHOLE = Ellipsis


def on_device(tile_u, tile_v, tile_ranks, lower_inverse, upper_inverse, row_order, sketch):
    size, width = sketch.shape
    count = len(ALL)
    ranks = tile_ranks.reshape(count)
    keep = (jnp.arange(width, dtype=jnp.int32)[None, :] < ranks[:, None])[:, None, :]
    u = tile_u.reshape(count, size, width)
    v = tile_v.reshape(count, size, width)
    places = jnp.stack([lax.axis_index(ROW), lax.axis_index(COL)]).astype(jnp.int32)
    last = jnp.stack([lax.axis_index("core"), lax.axis_index("y")]).astype(jnp.int32)
    info = jnp.concatenate([places, ranks, last])
    spots = jnp.arange(size, dtype=jnp.int32)

    pieces = [jnp.where(keep[n], x[n], 0) for x in (u, v) for n in (0, 1)]
    parts = spread_row(pieces, 0)
    half, other = spread_col(
        jnp.where(keep[0::2], u[0::2], 0), jnp.where(keep[0::2], v[0::2], 0), 0
    )
    flat = {tile: (0, n) for n, tile in enumerate(ALL)}
    pick = (row_order[:, :, None] == spots[None, None, :]).astype(BF16)
    lower = jnp.einsum("kap,kpb->kab", lower_inverse, pick, preferred_element_type=F32).astype(BF16)
    shared = (parts, half, other, lower, upper_inverse, sketch)
    sends = {
        (0, 0): ([(0, WHOLE), (4, 0)], [(2, WHOLE), (5, 0)]),
        (0, 1): ([(1, WHOLE)], [(3, WHOLE)]),
        (1, 0): ([(4, 1)], [(5, 1)]),
        (2, 0): ([(4, 2)], [(5, 2)]),
    }
    *pieces, side_u, side_v = compress(
        0, HEAD, flat, sends, (0, 0, 0, 0, 3, 3), info, (u,), (v,), *shared
    )
    parts = spread_row(pieces, 1)
    half, other = spread_col(side_u, side_v, 1)
    sends = {tile: ([(0, n)], [(1, n)]) for n, tile in enumerate(INNER)}
    inner_u, inner_v = compress(
        0, INNER, flat, sends, (2, 2), info, (u,), (v,), *shared
    )
    split = {
        (0, 0): (0, 0),
        (1, 0): (0, 1),
        (2, 0): (0, 2),
        (0, 1): (1, WHOLE),
        (1, 1): (2, 0),
        (2, 1): (2, 1),
    }
    sends = {tile: ([(0, n)], [(1, n)]) for n, tile in enumerate(ALL)}
    shared = (parts, half, other, lower, upper_inverse, sketch)
    ours = ((side_u, pieces[1], inner_u), (side_v, pieces[3], inner_v))
    u, v = compress(1, ALL, split, sends, (count, count), info, *ours, *shared)
    return u.reshape(tile_u.shape), v.reshape(tile_v.shape)


def solution(mesh):
    split = Mesh(mesh.devices.reshape(4, 8, 4, 2), ("y", "z", "x", "core"))
    tiles = P(None, ROW, None, COL, None, None)
    return jax.shard_map(
        on_device,
        mesh=split,
        in_specs=(tiles, tiles, P(None, ROW, None, COL), P(), P(), P(), P()),
        out_specs=(tiles, tiles),
        check_vma=False,
    )
```

profile of v0, /device:TPU:104, one launch (start us, length us, event | category | flops | bytes accessed | tf_op | source)
XLA Modules:
  0.0 123.3 jit_solution(16958805302868339438)
XLA Ops:
  2.8 1.8 %collective-permute-start.10 = (bf16[3,512,128]{2,1,0:T(8,128)(2,1)S(1)}, bf16[3,512,128]{2,1,0:T(8,128)(2,1)S(1)}, u32[]{:S(2)}, u32[]{:S(2)}) collective-permute-start(bf16[3,512,128]{2,1,0:T(8,128)(2,1)S(1)} %slice_select_fusion), channel_id=1, source_target_pairs={{0,1},{8,9},{16,17},{24,25},{32,33},{40,41},{48,49},{56,57},{64,65... | collective-permute-start | bytes 1179656 | tf_op jit(solution)/shard_map/ppermute | solution.py:279
  5.9 2.4 %collective-permute-start.12 = (bf16[3,512,128]{2,1,0:T(8,128)(2,1)S(1)}, bf16[3,512,128]{2,1,0:T(8,128)(2,1)S(1)}, u32[]{:S(2)}, u32[]{:S(2)}) collective-permute-start(bf16[3,512,128]{2,1,0:T(8,128)(2,1)S(1)} %select_select_fusion.1), channel_id=1, source_target_pairs={{0,6},{1,7},{8,14},{9,15},{16,22},{17,23},{24,30},{25,31},{32,38},... | collective-permute-start | bytes 1179656 | tf_op jit(solution)/shard_map/ppermute | solution.py:281
  8.4 2.1 %collective-permute-start.11 = (bf16[3,512,128]{2,1,0:T(8,128)(2,1)S(1)}, bf16[3,512,128]{2,1,0:T(8,128)(2,1)}, u32[]{:S(2)}, u32[]{:S(2)}) collective-permute-start(bf16[3,512,128]{2,1,0:T(8,128)(2,1)S(1)} %select_select_fusion.1), channel_id=1, source_target_pairs={{0,2},{1,3},{8,10},{9,11},{16,18},{17,19},{24,26},{25,27},{32,34},... | collective-permute-start | bytes 1179656 | tf_op jit(solution)/shard_map/ppermute | solution.py:281
  11.8 1.3 %collective-permute-start.2 = (bf16[512,128]{1,0:T(8,128)(2,1)}, bf16[512,128]{1,0:T(8,128)(2,1)}, u32[]{:S(2)}, u32[]{:S(2)}) collective-permute-start(bf16[512,128]{1,0:T(8,128)(2,1)} %get-tuple-element.27), channel_id=1, source_target_pairs={{0,192},{1,193},{2,194},{3,195},{4,196},{5,197},{6,198},{7,199}} | collective-permute-start | bytes 393224 | tf_op jit(solution)/shard_map/ppermute | solution.py:256
  13.2 1.3 %collective-permute-start = (bf16[512,128]{1,0:T(8,128)(2,1)}, bf16[512,128]{1,0:T(8,128)(2,1)}, u32[]{:S(2)}, u32[]{:S(2)}) collective-permute-start(bf16[512,128]{1,0:T(8,128)(2,1)} %get-tuple-element.34), channel_id=1, source_target_pairs={{0,64},{1,65},{2,66},{3,67},{4,68},{5,69},{6,70},{7,71}} | collective-permute-start | bytes 393224 | tf_op jit(solution)/shard_map/ppermute | solution.py:256
  16.1 1.3 %collective-permute-start.3 = (bf16[512,128]{1,0:T(8,128)(2,1)S(1)}, bf16[512,128]{1,0:T(8,128)(2,1)S(1)}, u32[]{:S(2)}, u32[]{:S(2)}) collective-permute-start(bf16[512,128]{1,0:T(8,128)(2,1)S(1)} %fusion.11), channel_id=1, source_target_pairs={{0,24},{64,88},{128,152},{192,216},{1,25},{65,89},{129,153},{193,2... | collective-permute-start | bytes 393224 | tf_op jit(solution)/shard_map/ppermute | solution.py:265
  20.5 8.4 %collective-permute-done.3 = bf16[512,128]{1,0:T(8,128)(2,1)S(1)} collective-permute-done((bf16[512,128]{1,0:T(8,128)(2,1)S(1)}, bf16[512,128]{1,0:T(8,128)(2,1)S(1)}, u32[]{:S(2)}, u32[]{:S(2)}) %collective-permute-start.3) | collective-permute-done | bytes 131104 | tf_op jit(solution)/shard_map/ppermute | solution.py:265
  28.9 1.3 %collective-permute-start.6 = (bf16[512,128]{1,0:T(8,128)(2,1)S(1)}, bf16[512,128]{1,0:T(8,128)(2,1)S(1)}, u32[]{:S(2)}, u32[]{:S(2)}) collective-permute-start(bf16[512,128]{1,0:T(8,128)(2,1)S(1)} %add_add_fusion.6), channel_id=1, source_target_pairs={{0,56},{24,16},{64,120},{88,80},{128,184},{152,144},{192,248},{216... | collective-permute-start | bytes 393224 | tf_op jit(solution)/shard_map/ppermute | solution.py:265
  30.3 1.3 %collective-permute-start.5 = (bf16[512,128]{1,0:T(8,128)(2,1)S(1)}, bf16[512,128]{1,0:T(8,128)(2,1)S(1)}, u32[]{:S(2)}, u32[]{:S(2)}) collective-permute-start(bf16[512,128]{1,0:T(8,128)(2,1)S(1)} %add_add_fusion.6), channel_id=1, source_target_pairs={{0,8},{24,32},{40,48},{64,72},{88,96},{104,112},{128,136},{152,160... | collective-permute-start | bytes 393224 | tf_op jit(solution)/shard_map/ppermute | solution.py:265
  32.8 1.3 %collective-permute-done.5 = bf16[512,128]{1,0:T(8,128)(2,1)S(1)} collective-permute-done((bf16[512,128]{1,0:T(8,128)(2,1)S(1)}, bf16[512,128]{1,0:T(8,128)(2,1)S(1)}, u32[]{:S(2)}, u32[]{:S(2)}) %collective-permute-start.5) | collective-permute-done | bytes 131104 | tf_op jit(solution)/shard_map/ppermute | solution.py:265
  34.4 1.4 %collective-permute-start.8 = (bf16[512,128]{1,0:T(8,128)(2,1)S(1)}, bf16[512,128]{1,0:T(8,128)(2,1)}, u32[]{:S(2)}, u32[]{:S(2)}) collective-permute-start(bf16[512,128]{1,0:T(8,128)(2,1)S(1)} %add_add_fusion.5.refs_2_), channel_id=1, source_target_pairs={{128,0},{192,64},{0,128},{64,192},{129,1},{193,65},{1,129},{65,193... | collective-permute-start | bytes 393224 | tf_op jit(solution)/shard_map/ppermute | solution.py:271
  35.8 1.9 %collective-permute-start.7 = (bf16[512,128]{1,0:T(8,128)(2,1)S(1)}, bf16[512,128]{1,0:T(8,128)(2,1)}, u32[]{:S(2)}, u32[]{:S(2)}) collective-permute-start(bf16[512,128]{1,0:T(8,128)(2,1)S(1)} %add_add_fusion.5.refs_2_), channel_id=1, source_target_pairs={{64,0},{128,64},{192,128},{0,192},{65,1},{129,65},{193,129},{1,193... | collective-permute-start | bytes 393224 | tf_op jit(solution)/shard_map/ppermute | solution.py:271
  37.7 1.8 %fusion.2.refs_8_.refs_12_ = bf16[2,512,512]{2,1,0:T(8,128)(2,1)} fusion(bf16[2,512,512]{2,1,0:T(8,128)(2,1)S(1)} %copy-done, s32[2,512]{1,0:T(2,128)S(1)} %copy-done.13), kind=kOutput, calls=%fused_computation.3 | convolution fusion | flops 537919488 | bytes 2101248 | tf_op jit(solution)/shard_map/kap,kpb->kab/dot_general | solution.py:316
  39.6 1.5 %collective-permute-done.8.refs_4_ = bf16[512,128]{1,0:T(8,128)(2,1)} collective-permute-done((bf16[512,128]{1,0:T(8,128)(2,1)S(1)}, bf16[512,128]{1,0:T(8,128)(2,1)}, u32[]{:S(2)}, u32[]{:S(2)}) %collective-permute-start.8) | collective-permute-done | bytes 131104 | tf_op jit(solution)/shard_map/ppermute | solution.py:271
  43.0 1.2 copy-done.3
  44.3 1.2 copy-done.5
  47.4 11.7 %shard_map.86 = (bf16[512,128]{1,0:T(8,128)(2,1)S(1)}, bf16[512,128]{1,0:T(8,128)(2,1)}, bf16[512,128]{1,0:T(8,128)(2,1)}, bf16[512,128]{1,0:T(8,128)(2,1)}, bf1...) custom-call(s32[10]{0:T(128)S(1)} %concatenate.9.info, bf16[6,512,128]{2,1,0:T(8,128)(2,1)S(1)} %bitcast.49, ...), custom_call_target="tpu_custom_call" | custom-call | flops 2013265920 | bytes 2097152 | tf_op jit(solution)/shard_map/pallas_call | solution.py:222
  59.7 1.3 %collective-permute-start.26 = (bf16[3,512,128]{2,1,0:T(8,128)(2,1)}, bf16[3,512,128]{2,1,0:T(8,128)(2,1)}, u32[]{:S(2)}, u32[]{:S(2)}) collective-permute-start(bf16[3,512,128]{2,1,0:T(8,128)(2,1)} %get-tuple-element.12.refs_0_), channel_id=1, source_target_pairs={{1,0},{9,8},{17,16},{25,24},{33,32},{41,40},{49,48},{57,56},{65,64... | collective-permute-start | bytes 1179656 | tf_op jit(solution)/shard_map/ppermute | solution.py:279
  61.0 2.7 %collective-permute-done.26 = bf16[3,512,128]{2,1,0:T(8,128)(2,1)} collective-permute-done((bf16[3,512,128]{2,1,0:T(8,128)(2,1)}, bf16[3,512,128]{2,1,0:T(8,128)(2,1)}, u32[]{:S(2)}, u32[]{:S(2)}) %collective-permute-start.26) | collective-permute-done | bytes 393248 | tf_op jit(solution)/shard_map/ppermute | solution.py:279
  63.7 1.8 %select_select_fusion = bf16[3,512,128]{2,1,0:T(8,128)(2,1)} fusion(bf16[3,512,128]{2,1,0:T(8,128)(2,1)S(1)} %get-tuple-element.15.refs_3_, bf16[3,512,128]{2,1,0:T(8,128)(2,1)} %collective-permute-done.26, pred[]{:T(512)S(6)} %eq.41, pred[]{:T(512)S(6)} %eq.35), kind=kLoop, calls=%fused_computation.8 | loop fusion | flops 393216 | bytes 1179650 | tf_op jit(solution)/shard_map/jit(_where)/select_n | solution.py:280
  65.4 2.0 %collective-permute-start.28 = (bf16[3,512,128]{2,1,0:T(8,128)(2,1)}, bf16[3,512,128]{2,1,0:T(8,128)(2,1)}, u32[]{:S(2)}, u32[]{:S(2)}) collective-permute-start(bf16[3,512,128]{2,1,0:T(8,128)(2,1)} %select_select_fusion), channel_id=1, source_target_pairs={{0,6},{1,7},{8,14},{9,15},{16,22},{17,23},{24,30},{25,31},{32,38},... | collective-permute-start | bytes 1179656 | tf_op jit(solution)/shard_map/ppermute | solution.py:281
  67.5 2.1 %collective-permute-start.27 = (bf16[3,512,128]{2,1,0:T(8,128)(2,1)}, bf16[3,512,128]{2,1,0:T(8,128)(2,1)}, u32[]{:S(2)}, u32[]{:S(2)}) collective-permute-start(bf16[3,512,128]{2,1,0:T(8,128)(2,1)} %select_select_fusion), channel_id=1, source_target_pairs={{0,2},{1,3},{8,10},{9,11},{16,18},{17,19},{24,26},{25,27},{32,34},... | collective-permute-start | bytes 1179656 | tf_op jit(solution)/shard_map/ppermute | solution.py:281
  69.5 1.3 %collective-permute-start.17 = (bf16[512,128]{1,0:T(8,128)(2,1)}, bf16[512,128]{1,0:T(8,128)(2,1)}, u32[]{:S(2)}, u32[]{:S(2)}) collective-permute-start(bf16[512,128]{1,0:T(8,128)(2,1)} %get-tuple-element.19), channel_id=1, source_target_pairs={{8,136},{9,137},{10,138},{11,139},{12,140},{13,141},{14,142},{15,1... | collective-permute-start | bytes 393224 | tf_op jit(solution)/shard_map/ppermute | solution.py:256
  70.8 1.3 %collective-permute-start.16 = (bf16[512,128]{1,0:T(8,128)(2,1)}, bf16[512,128]{1,0:T(8,128)(2,1)}, u32[]{:S(2)}, u32[]{:S(2)}) collective-permute-start(bf16[512,128]{1,0:T(8,128)(2,1)} %get-tuple-element.13.refs_1_), channel_id=1, source_target_pairs={{8,72},{9,73},{10,74},{11,75},{12,76},{13,77},{14,78},{15,79}} | collective-permute-start | bytes 393224 | tf_op jit(solution)/shard_map/ppermute | solution.py:256
  72.1 1.3 %collective-permute-start.18 = (bf16[512,128]{1,0:T(8,128)(2,1)}, bf16[512,128]{1,0:T(8,128)(2,1)}, u32[]{:S(2)}, u32[]{:S(2)}) collective-permute-start(bf16[512,128]{1,0:T(8,128)(2,1)} %get-tuple-element.16.refs_4_), channel_id=1, source_target_pairs={{8,200},{9,201},{10,202},{11,203},{12,204},{13,205},{14,206},{15,2... | collective-permute-start | bytes 393224 | tf_op jit(solution)/shard_map/ppermute | solution.py:256
  77.0 1.3 %add_add_fusion = bf16[3,512,128]{2,1,0:T(8,128)(2,1)S(1)} fusion(bf16[3,512,128]{2,1,0:T(8,128)(2,1)} %collective-permute-done.28, bf16[3,512,128]{2,1,0:T(8,128)(2,1)} %select_select_fusion, bf16[3,512,128]{2,1,0:T(8,128)(2,1)} %collective-permute-done.27), kind=kLoop, calls=%fused_computation.7 | loop fusion | flops 393216 | bytes 1572864 | tf_op jit(solution)/shard_map/add | solution.py:282
  80.1 1.3 %collective-permute-start.22 = (bf16[512,128]{1,0:T(8,128)(2,1)S(1)}, bf16[512,128]{1,0:T(8,128)(2,1)S(1)}, u32[]{:S(2)}, u32[]{:S(2)}) collective-permute-start(bf16[512,128]{1,0:T(8,128)(2,1)S(1)} %add_add_fusion.3), channel_id=1, source_target_pairs={{8,0},{32,24},{72,64},{96,88},{136,128},{160,152},{200,192},{224,2... | collective-permute-start | bytes 393224 | tf_op jit(solution)/shard_map/ppermute | solution.py:265
  82.3 12.1 %collective-permute-done.22 = bf16[512,128]{1,0:T(8,128)(2,1)S(1)} collective-permute-done((bf16[512,128]{1,0:T(8,128)(2,1)S(1)}, bf16[512,128]{1,0:T(8,128)(2,1)S(1)}, u32[]{:S(2)}, u32[]{:S(2)}) %collective-permute-start.22) | collective-permute-done | bytes 131104 | tf_op jit(solution)/shard_map/ppermute | solution.py:265
  94.5 3.4 %collective-permute-start.24 = (bf16[512,128]{1,0:T(8,128)(2,1)S(1)}, bf16[512,128]{1,0:T(8,128)(2,1)S(1)}, u32[]{:S(2)}, u32[]{:S(2)}) collective-permute-start(bf16[512,128]{1,0:T(8,128)(2,1)S(1)} %add_add_fusion.2.refs_6_), channel_id=1, source_target_pairs={{128,0},{192,64},{0,128},{64,192},{129,1},{193,65},{1,129},{65,193... | collective-permute-start | bytes 393224 | tf_op jit(solution)/shard_map/ppermute | solution.py:271
  98.0 2.3 %collective-permute-start.23 = (bf16[512,128]{1,0:T(8,128)(2,1)S(1)}, bf16[512,128]{1,0:T(8,128)(2,1)S(1)}, u32[]{:S(2)}, u32[]{:S(2)}) collective-permute-start(bf16[512,128]{1,0:T(8,128)(2,1)S(1)} %add_add_fusion.2.refs_6_), channel_id=1, source_target_pairs={{64,0},{128,64},{192,128},{0,192},{65,1},{129,65},{193,129},{1,193... | collective-permute-start | bytes 393224 | tf_op jit(solution)/shard_map/ppermute | solution.py:271
  100.3 7.6 %shard_map.87 = (bf16[2,512,128]{2,1,0:T(8,128)(2,1)S(1)}, bf16[2,512,128]{2,1,0:T(8,128)(2,1)S(1)}) custom-call(s32[10]{0:T(128)S(1)} %concatenate.9.info, bf16[6,512,128]{2,1,0:T(8,128)(2,1)S(1)} %bitcast.50, bf16[6,512,128]{2,1,0:T(8,128)(2,1)S(1)} %bitcast.54, bf16[512,128]{1,0:T(8,128)(2,1)S(1)} %add_add_fusion.5.refs_2_, ...), custom_call_target="tpu_custom_call" | custom-call | flops 1006632960 | bytes 1048576 | tf_op jit(solution)/shard_map/pallas_call | solution.py:222
  108.0 15.3 %shard_map.88 = (bf16[6,512,128]{2,1,0:T(8,128)(2,1)}, bf16[6,512,128]{2,1,0:T(8,128)(2,1)}) custom-call(s32[10]{0:T(128)S(1)} %concatenate.9.info, bf16[3,512,128]{2,1,0:T(8,128)(2,1)} %get-tuple-element.12.refs_0_, bf16[512,128]{1,0:T(8,128)(2,1)} %get-tuple-element.13.refs_1_, bf16[2,512,128]{2,1,0:T(8,128)(2,1)S(1)} %get-tuple-element.14.refs_2_, ...), custom_call_target="tpu_custom_call" | custom-call | flops 3019898880 | bytes 3145728 | tf_op jit(solution)/shard_map/pallas_call | solution.py:222
  (87 shorter events, 21.9 us)
Async XLA Ops:
  2.8 3.1 %collective-permute-start.10 = (bf16[3,512,128]{2,1,0:T(8,128)(2,1)S(1)}, bf16[3,512,128]{2,1,0:T(8,128)(2,1)S(1)}, u32[]{:S(2)}, u32[]{:S(2)}) collective-permute-start(bf16[3,512,128]{2,1,0:T(8,128)(2,1)S(1)} %slice_select_fusion), channel_id=1, source_target_pairs={{0,1},{8,9},{16,17},{24,25},{32,33},{40,41},{48,49},{56,57},{64,65... | collective-permute-start | bytes 1179656 | tf_op jit(solution)/shard_map/ppermute | solution.py:279
  5.9 11.5 %collective-permute-start.12 = (bf16[3,512,128]{2,1,0:T(8,128)(2,1)S(1)}, bf16[3,512,128]{2,1,0:T(8,128)(2,1)S(1)}, u32[]{:S(2)}, u32[]{:S(2)}) collective-permute-start(bf16[3,512,128]{2,1,0:T(8,128)(2,1)S(1)} %select_select_fusion.1), channel_id=1, source_target_pairs={{0,6},{1,7},{8,14},{9,15},{16,22},{17,23},{24,30},{25,31},{32,38},... | collective-permute-start | bytes 1179656 | tf_op jit(solution)/shard_map/ppermute | solution.py:281
  8.4 9.7 %collective-permute-start.11 = (bf16[3,512,128]{2,1,0:T(8,128)(2,1)S(1)}, bf16[3,512,128]{2,1,0:T(8,128)(2,1)}, u32[]{:S(2)}, u32[]{:S(2)}) collective-permute-start(bf16[3,512,128]{2,1,0:T(8,128)(2,1)S(1)} %select_select_fusion.1), channel_id=1, source_target_pairs={{0,2},{1,3},{8,10},{9,11},{16,18},{17,19},{24,26},{25,27},{32,34},... | collective-permute-start | bytes 1179656 | tf_op jit(solution)/shard_map/ppermute | solution.py:281
  11.2 3.3 %collective-permute-start.1 = (bf16[512,128]{1,0:T(8,128)(2,1)}, bf16[512,128]{1,0:T(8,128)(2,1)S(1)}, u32[]{:S(2)}, u32[]{:S(2)}) collective-permute-start(bf16[512,128]{1,0:T(8,128)(2,1)} %get-tuple-element.26), channel_id=1, source_target_pairs={{0,128},{1,129},{2,130},{3,131},{4,132},{5,133},{6,134},{7,135}} | collective-permute-start | bytes 393224 | tf_op jit(solution)/shard_map/ppermute | solution.py:256
  11.8 2.6 %collective-permute-start.2 = (bf16[512,128]{1,0:T(8,128)(2,1)}, bf16[512,128]{1,0:T(8,128)(2,1)}, u32[]{:S(2)}, u32[]{:S(2)}) collective-permute-start(bf16[512,128]{1,0:T(8,128)(2,1)} %get-tuple-element.27), channel_id=1, source_target_pairs={{0,192},{1,193},{2,194},{3,195},{4,196},{5,197},{6,198},{7,199}} | collective-permute-start | bytes 393224 | tf_op jit(solution)/shard_map/ppermute | solution.py:256
  13.2 1.3 %collective-permute-start = (bf16[512,128]{1,0:T(8,128)(2,1)}, bf16[512,128]{1,0:T(8,128)(2,1)}, u32[]{:S(2)}, u32[]{:S(2)}) collective-permute-start(bf16[512,128]{1,0:T(8,128)(2,1)} %get-tuple-element.34), channel_id=1, source_target_pairs={{0,64},{1,65},{2,66},{3,67},{4,68},{5,69},{6,70},{7,71}} | collective-permute-start | bytes 393224 | tf_op jit(solution)/shard_map/ppermute | solution.py:256
  15.5 5.0 %collective-permute-start.4 = (bf16[512,128]{1,0:T(8,128)(2,1)S(1)}, bf16[512,128]{1,0:T(8,128)(2,1)S(1)}, u32[]{:S(2)}, u32[]{:S(2)}) collective-permute-start(bf16[512,128]{1,0:T(8,128)(2,1)S(1)} %fusion.11), channel_id=1, source_target_pairs={{0,40},{64,104},{128,168},{192,232},{1,41},{65,105},{129,169},{193... | collective-permute-start | bytes 393224 | tf_op jit(solution)/shard_map/ppermute | solution.py:265
  16.1 12.8 %collective-permute-start.3 = (bf16[512,128]{1,0:T(8,128)(2,1)S(1)}, bf16[512,128]{1,0:T(8,128)(2,1)S(1)}, u32[]{:S(2)}, u32[]{:S(2)}) collective-permute-start(bf16[512,128]{1,0:T(8,128)(2,1)S(1)} %fusion.11), channel_id=1, source_target_pairs={{0,24},{64,88},{128,152},{192,216},{1,25},{65,89},{129,153},{193,2... | collective-permute-start | bytes 393224 | tf_op jit(solution)/shard_map/ppermute | solution.py:265
  19.1 12.5 %collective-permute-start.13 = (bf16[3,256,128]{2,1,0:T(8,128)(2,1)S(1)}, bf16[3,256,128]{2,1,0:T(8,128)(2,1)S(1)}, u32[]{:S(2)}, u32[]{:S(2)}) collective-permute-start(bf16[3,256,128]{2,1,0:T(8,128)(2,1)S(1)} %get-tuple-element.30), channel_id=1, source_target_pairs={{2,4},{3,5},{10,12},{11,13},{18,20},{19,21},{26,28},{27,29},{34,36... | collective-permute-start | bytes 589832 | tf_op jit(solution)/shard_map/ppermute | solution.py:284
  19.8 11.8 %collective-permute-start.14 = (bf16[3,256,128]{2,1,0:T(8,128)(2,1)S(1)}, bf16[3,256,128]{2,1,0:T(8,128)(2,1)S(1)}, u32[]{:S(2)}, u32[]{:S(2)}) collective-permute-start(bf16[3,256,128]{2,1,0:T(8,128)(2,1)S(1)} %get-tuple-element.31), channel_id=1, source_target_pairs={{6,4},{7,5},{14,12},{15,13},{22,20},{23,21},{30,28},{31,29},{38,36... | collective-permute-start | bytes 589832 | tf_op jit(solution)/shard_map/ppermute | solution.py:285
  28.9 3.8 %collective-permute-start.6 = (bf16[512,128]{1,0:T(8,128)(2,1)S(1)}, bf16[512,128]{1,0:T(8,128)(2,1)S(1)}, u32[]{:S(2)}, u32[]{:S(2)}) collective-permute-start(bf16[512,128]{1,0:T(8,128)(2,1)S(1)} %add_add_fusion.6), channel_id=1, source_target_pairs={{0,56},{24,16},{64,120},{88,80},{128,184},{152,144},{192,248},{216... | collective-permute-start | bytes 393224 | tf_op jit(solution)/shard_map/ppermute | solution.py:265
  30.3 3.8 %collective-permute-start.5 = (bf16[512,128]{1,0:T(8,128)(2,1)S(1)}, bf16[512,128]{1,0:T(8,128)(2,1)S(1)}, u32[]{:S(2)}, u32[]{:S(2)}) collective-permute-start(bf16[512,128]{1,0:T(8,128)(2,1)S(1)} %add_add_fusion.6), channel_id=1, source_target_pairs={{0,8},{24,32},{40,48},{64,72},{88,96},{104,112},{128,136},{152,160... | collective-permute-start | bytes 393224 | tf_op jit(solution)/shard_map/ppermute | solution.py:265
  31.7 10.6 %collective-permute-start.15 = (bf16[3,512,128]{2,1,0:T(8,128)(2,1)S(1)}, bf16[3,512,128]{2,1,0:T(8,128)(2,1)S(1)}, u32[]{:S(2)}, u32[]{:S(2)}) collective-permute-start(bf16[3,512,128]{2,1,0:T(8,128)(2,1)S(1)} %maximum_add_fusion.refs_6_), channel_id=1, source_target_pairs={{0,1},{1,0},{2,3},{3,2},{4,5},{5,4},{6,7},{7,6},{8,9},{9,8},{10,11... | collective-permute-start | bytes 1179656 | tf_op jit(solution)/shard_map/ppermute | solution.py:287
  34.1 5.5 %collective-permute-start.9 = (bf16[512,128]{1,0:T(8,128)(2,1)S(1)}, bf16[512,128]{1,0:T(8,128)(2,1)}, u32[]{:S(2)}, u32[]{:S(2)}) collective-permute-start(bf16[512,128]{1,0:T(8,128)(2,1)S(1)} %add_add_fusion.5.refs_2_), channel_id=1, source_target_pairs={{192,0},{0,64},{64,128},{128,192},{193,1},{1,65},{65,129},{129,193... | collective-permute-start | bytes 393224 | tf_op jit(solution)/shard_map/ppermute | solution.py:271
  34.4 6.7 %collective-permute-start.8 = (bf16[512,128]{1,0:T(8,128)(2,1)S(1)}, bf16[512,128]{1,0:T(8,128)(2,1)}, u32[]{:S(2)}, u32[]{:S(2)}) collective-permute-start(bf16[512,128]{1,0:T(8,128)(2,1)S(1)} %add_add_fusion.5.refs_2_), channel_id=1, source_target_pairs={{128,0},{192,64},{0,128},{64,192},{129,1},{193,65},{1,129},{65,193... | collective-permute-start | bytes 393224 | tf_op jit(solution)/shard_map/ppermute | solution.py:271
  35.8 6.5 %collective-permute-start.7 = (bf16[512,128]{1,0:T(8,128)(2,1)S(1)}, bf16[512,128]{1,0:T(8,128)(2,1)}, u32[]{:S(2)}, u32[]{:S(2)}) collective-permute-start(bf16[512,128]{1,0:T(8,128)(2,1)S(1)} %add_add_fusion.5.refs_2_), channel_id=1, source_target_pairs={{64,0},{128,64},{192,128},{0,192},{65,1},{129,65},{193,129},{1,193... | collective-permute-start | bytes 393224 | tf_op jit(solution)/shard_map/ppermute | solution.py:271
  59.7 3.9 %collective-permute-start.26 = (bf16[3,512,128]{2,1,0:T(8,128)(2,1)}, bf16[3,512,128]{2,1,0:T(8,128)(2,1)}, u32[]{:S(2)}, u32[]{:S(2)}) collective-permute-start(bf16[3,512,128]{2,1,0:T(8,128)(2,1)} %get-tuple-element.12.refs_0_), channel_id=1, source_target_pairs={{1,0},{9,8},{17,16},{25,24},{33,32},{41,40},{49,48},{57,56},{65,64... | collective-permute-start | bytes 1179656 | tf_op jit(solution)/shard_map/ppermute | solution.py:279
  65.4 10.5 %collective-permute-start.28 = (bf16[3,512,128]{2,1,0:T(8,128)(2,1)}, bf16[3,512,128]{2,1,0:T(8,128)(2,1)}, u32[]{:S(2)}, u32[]{:S(2)}) collective-permute-start(bf16[3,512,128]{2,1,0:T(8,128)(2,1)} %select_select_fusion), channel_id=1, source_target_pairs={{0,6},{1,7},{8,14},{9,15},{16,22},{17,23},{24,30},{25,31},{32,38},... | collective-permute-start | bytes 1179656 | tf_op jit(solution)/shard_map/ppermute | solution.py:281
  67.5 9.5 %collective-permute-start.27 = (bf16[3,512,128]{2,1,0:T(8,128)(2,1)}, bf16[3,512,128]{2,1,0:T(8,128)(2,1)}, u32[]{:S(2)}, u32[]{:S(2)}) collective-permute-start(bf16[3,512,128]{2,1,0:T(8,128)(2,1)} %select_select_fusion), channel_id=1, source_target_pairs={{0,2},{1,3},{8,10},{9,11},{16,18},{17,19},{24,26},{25,27},{32,34},... | collective-permute-start | bytes 1179656 | tf_op jit(solution)/shard_map/ppermute | solution.py:281
  69.5 3.9 %collective-permute-start.17 = (bf16[512,128]{1,0:T(8,128)(2,1)}, bf16[512,128]{1,0:T(8,128)(2,1)}, u32[]{:S(2)}, u32[]{:S(2)}) collective-permute-start(bf16[512,128]{1,0:T(8,128)(2,1)} %get-tuple-element.19), channel_id=1, source_target_pairs={{8,136},{9,137},{10,138},{11,139},{12,140},{13,141},{14,142},{15,1... | collective-permute-start | bytes 393224 | tf_op jit(solution)/shard_map/ppermute | solution.py:256
  70.8 2.6 %collective-permute-start.16 = (bf16[512,128]{1,0:T(8,128)(2,1)}, bf16[512,128]{1,0:T(8,128)(2,1)}, u32[]{:S(2)}, u32[]{:S(2)}) collective-permute-start(bf16[512,128]{1,0:T(8,128)(2,1)} %get-tuple-element.13.refs_1_), channel_id=1, source_target_pairs={{8,72},{9,73},{10,74},{11,75},{12,76},{13,77},{14,78},{15,79}} | collective-permute-start | bytes 393224 | tf_op jit(solution)/shard_map/ppermute | solution.py:256
  72.1 1.3 %collective-permute-start.18 = (bf16[512,128]{1,0:T(8,128)(2,1)}, bf16[512,128]{1,0:T(8,128)(2,1)}, u32[]{:S(2)}, u32[]{:S(2)}) collective-permute-start(bf16[512,128]{1,0:T(8,128)(2,1)} %get-tuple-element.16.refs_4_), channel_id=1, source_target_pairs={{8,200},{9,201},{10,202},{11,203},{12,204},{13,205},{14,206},{15,2... | collective-permute-start | bytes 393224 | tf_op jit(solution)/shard_map/ppermute | solution.py:256
  74.5 5.5 %collective-permute-start.20 = (bf16[512,128]{1,0:T(8,128)(2,1)S(1)}, bf16[512,128]{1,0:T(8,128)(2,1)S(1)}, u32[]{:S(2)}, u32[]{:S(2)}) collective-permute-start(bf16[512,128]{1,0:T(8,128)(2,1)S(1)} %add_add_fusion.4), channel_id=1, source_target_pairs={{8,48},{72,112},{136,176},{200,240},{9,49},{73,113},{137,177},{201... | collective-permute-start | bytes 393224 | tf_op jit(solution)/shard_map/ppermute | solution.py:265
  75.2 4.8 %collective-permute-start.19 = (bf16[512,128]{1,0:T(8,128)(2,1)S(1)}, bf16[512,128]{1,0:T(8,128)(2,1)S(1)}, u32[]{:S(2)}, u32[]{:S(2)}) collective-permute-start(bf16[512,128]{1,0:T(8,128)(2,1)S(1)} %add_add_fusion.4), channel_id=1, source_target_pairs={{8,32},{72,96},{136,160},{200,224},{9,33},{73,97},{137,161},{201,2... | collective-permute-start | bytes 393224 | tf_op jit(solution)/shard_map/ppermute | solution.py:265
  78.4 3.7 %collective-permute-start.29 = (bf16[3,256,128]{2,1,0:T(8,128)(2,1)S(1)}, bf16[3,256,128]{2,1,0:T(8,128)(2,1)S(1)}, u32[]{:S(2)}, u32[]{:S(2)}) collective-permute-start(bf16[3,256,128]{2,1,0:T(8,128)(2,1)S(1)} %get-tuple-element.28), channel_id=1, source_target_pairs={{2,4},{3,5},{10,12},{11,13},{18,20},{19,21},{26,28},{27,29},{34,36... | collective-permute-start | bytes 589832 | tf_op jit(solution)/shard_map/ppermute | solution.py:284
  79.2 2.9 %collective-permute-start.30 = (bf16[3,256,128]{2,1,0:T(8,128)(2,1)S(1)}, bf16[3,256,128]{2,1,0:T(8,128)(2,1)S(1)}, u32[]{:S(2)}, u32[]{:S(2)}) collective-permute-start(bf16[3,256,128]{2,1,0:T(8,128)(2,1)S(1)} %get-tuple-element.29), channel_id=1, source_target_pairs={{6,4},{7,5},{14,12},{15,13},{22,20},{23,21},{30,28},{31,29},{38,36... | collective-permute-start | bytes 589832 | tf_op jit(solution)/shard_map/ppermute | solution.py:285
  80.1 14.3 %collective-permute-start.22 = (bf16[512,128]{1,0:T(8,128)(2,1)S(1)}, bf16[512,128]{1,0:T(8,128)(2,1)S(1)}, u32[]{:S(2)}, u32[]{:S(2)}) collective-permute-start(bf16[512,128]{1,0:T(8,128)(2,1)S(1)} %add_add_fusion.3), channel_id=1, source_target_pairs={{8,0},{32,24},{72,64},{96,88},{136,128},{160,152},{200,192},{224,2... | collective-permute-start | bytes 393224 | tf_op jit(solution)/shard_map/ppermute | solution.py:265
  81.4 13.0 %collective-permute-start.21 = (bf16[512,128]{1,0:T(8,128)(2,1)S(1)}, bf16[512,128]{1,0:T(8,128)(2,1)S(1)}, u32[]{:S(2)}, u32[]{:S(2)}) collective-permute-start(bf16[512,128]{1,0:T(8,128)(2,1)S(1)} %add_add_fusion.3), channel_id=1, source_target_pairs={{8,16},{32,40},{48,56},{72,80},{96,104},{112,120},{136,144},{160,1... | collective-permute-start | bytes 393224 | tf_op jit(solution)/shard_map/ppermute | solution.py:265
  82.2 25.8 %collective-permute-start.31 = (bf16[3,512,128]{2,1,0:T(8,128)(2,1)S(1)}, bf16[3,512,128]{2,1,0:T(8,128)(2,1)S(1)}, u32[]{:S(2)}, u32[]{:S(2)}) collective-permute-start(bf16[3,512,128]{2,1,0:T(8,128)(2,1)S(1)} %maximum_add_fusion.1.refs_10_), channel_id=1, source_target_pairs={{0,1},{1,0},{2,3},{3,2},{4,5},{5,4},{6,7},{7,6},{8,9},{9,8},{10,11... | collective-permute-start | bytes 1179656 | tf_op jit(solution)/shard_map/ppermute | solution.py:287
  94.4 13.5 %collective-permute-start.25 = (bf16[512,128]{1,0:T(8,128)(2,1)S(1)}, bf16[512,128]{1,0:T(8,128)(2,1)S(1)}, u32[]{:S(2)}, u32[]{:S(2)}) collective-permute-start(bf16[512,128]{1,0:T(8,128)(2,1)S(1)} %add_add_fusion.2.refs_6_), channel_id=1, source_target_pairs={{192,0},{0,64},{64,128},{128,192},{193,1},{1,65},{65,129},{129,193... | collective-permute-start | bytes 393224 | tf_op jit(solution)/shard_map/ppermute | solution.py:271
  94.5 13.4 %collective-permute-start.24 = (bf16[512,128]{1,0:T(8,128)(2,1)S(1)}, bf16[512,128]{1,0:T(8,128)(2,1)S(1)}, u32[]{:S(2)}, u32[]{:S(2)}) collective-permute-start(bf16[512,128]{1,0:T(8,128)(2,1)S(1)} %add_add_fusion.2.refs_6_), channel_id=1, source_target_pairs={{128,0},{192,64},{0,128},{64,192},{129,1},{193,65},{1,129},{65,193... | collective-permute-start | bytes 393224 | tf_op jit(solution)/shard_map/ppermute | solution.py:271
  98.0 10.0 %collective-permute-start.23 = (bf16[512,128]{1,0:T(8,128)(2,1)S(1)}, bf16[512,128]{1,0:T(8,128)(2,1)S(1)}, u32[]{:S(2)}, u32[]{:S(2)}) collective-permute-start(bf16[512,128]{1,0:T(8,128)(2,1)S(1)} %add_add_fusion.2.refs_6_), channel_id=1, source_target_pairs={{64,0},{128,64},{192,128},{0,192},{65,1},{129,65},{193,129},{1,193... | collective-permute-start | bytes 393224 | tf_op jit(solution)/shard_map/ppermute | solution.py:271
  (14 other events, 161.0 us)
where the time goes:
time: 124 us; the launch traced here: 123 us
  starting transfers between devices  39.3 us (32%)
  Pallas kernels  34.7 us (28%)
  waiting for transfers between devices  31.1 us (25%)
  other arithmetic  8.47 us (7%)
  local copies, waits for them, and re-layouts  6.97 us (6%)
  matrix products  1.79 us (1%)
    pallas_call x3, Pallas kernels, compress(): pl.pallas_call(functools.partial(compress_kernel, panel_id, tiles, places...  34.7 us
    ppermute x8, waiting for transfers between devices, along_z(): return lax.ppermute(part, ROW, pairs)  22.8 us
    ppermute x6, starting transfers between devices, spread_row(): lax.ppermute(part, 'y', [((k + s) % n_y, k) for k in range(n_y)])  9.47 us
    ppermute x8, starting transfers between devices, along_z(): return lax.ppermute(part, ROW, pairs)  7.85 us
    ppermute x6, starting transfers between devices, spread_row(): lax.ppermute(pieces[k], ROW, [(root, k * n_z + root)])  7.21 us
    unnamed x29, local copies, waits for them, and re-layouts  6.7 us
    ppermute x2, starting transfers between devices, spread_col(): lax.ppermute(start, 'x', [(0, 3)])  4.44 us
    ppermute x2, starting transfers between devices, spread_col(): lax.ppermute(start, 'x', [(0, 1)])  4.11 us
  transfers between devices with their start and end apart: 32, of which 10 were waited for; matrix products, arithmetic and copies ran while one was open for 6% of the time, Pallas kernels for 6%

commit v1 on v0

--- a/solution.py
+++ b/solution.py
@@ -120,7 +120,7 @@
             top[k] = jnp.where(turn < 2, near, far)
     sk_t[...] = sketch[...].T
     for e in tops:
-        turned[e] = dot_nn(lp[panel_id], top[e]).astype(BF16)
+        turned[e] = dot_nn(lp[...], top[e]).astype(BF16)
     upper_t = upper[panel_id].T
     for a in lefts:
         side_u[a] = jnp.where(first_core, half[a], other[a])
@@ -205,10 +205,9 @@
             keep_v = jnp.where((col_place == panel_id) & (row_id > panel_id), side[a], keep_v)
         new_u = fresh_u if settled else jnp.where(chosen, fresh_u, keep_u)
         new_v = fresh_v if settled else jnp.where(chosen, fresh_v, keep_v)
-        for out, index in sends[a, e][0]:
-            outs[out][index] = new_u
-        for out, index in sends[a, e][1]:
-            outs[out][index] = new_v
+        for value, spots in zip((new_u, new_v), sends[a, e]):
+            for out, index in spots:
+                outs[out][index] = value
 
 
 def compress(
@@ -289,8 +288,6 @@
 
 
 ALL = ((0, 0), (0, 1), (1, 0), (1, 1), (2, 0), (2, 1))
-HEAD = ((0, 0), (0, 1), (1, 0), (2, 0))
-INNER = ((1, 1), (2, 1))
 WHOLE = Ellipsis
 
 
@@ -306,30 +303,30 @@
     info = jnp.concatenate([places, ranks, last])
     spots = jnp.arange(size, dtype=jnp.int32)
 
+    def turns(panel):
+        pick = (row_order[panel][:, None] == spots[None, :]).astype(BF16)
+        return dot_nn(lower_inverse[panel], pick).astype(BF16)
+
     pieces = [jnp.where(keep[n], x[n], 0) for x in (u, v) for n in (0, 1)]
     parts = spread_row(pieces, 0)
     half, other = spread_col(
         jnp.where(keep[0::2], u[0::2], 0), jnp.where(keep[0::2], v[0::2], 0), 0
     )
     flat = {tile: (0, n) for n, tile in enumerate(ALL)}
-    pick = (row_order[:, :, None] == spots[None, None, :]).astype(BF16)
-    lower = jnp.einsum("kap,kpb->kab", lower_inverse, pick, preferred_element_type=F32).astype(BF16)
-    shared = (parts, half, other, lower, upper_inverse, sketch)
+    shared = (parts, half, other, turns(0), upper_inverse, sketch)
     sends = {
         (0, 0): ([(0, WHOLE), (4, 0)], [(2, WHOLE), (5, 0)]),
         (0, 1): ([(1, WHOLE)], [(3, WHOLE)]),
         (1, 0): ([(4, 1)], [(5, 1)]),
         (2, 0): ([(4, 2)], [(5, 2)]),
+        (1, 1): ([(6, 0)], [(7, 0)]),
+        (2, 1): ([(6, 1)], [(7, 1)]),
     }
-    *pieces, side_u, side_v = compress(
-        0, HEAD, flat, sends, (0, 0, 0, 0, 3, 3), info, (u,), (v,), *shared
+    *pieces, side_u, side_v, inner_u, inner_v = compress(
+        0, ALL, flat, sends, (0, 0, 0, 0, 3, 3, 2, 2), info, (u,), (v,), *shared
     )
     parts = spread_row(pieces, 1)
     half, other = spread_col(side_u, side_v, 1)
-    sends = {tile: ([(0, n)], [(1, n)]) for n, tile in enumerate(INNER)}
-    inner_u, inner_v = compress(
-        0, INNER, flat, sends, (2, 2), info, (u,), (v,), *shared
-    )
     split = {
         (0, 0): (0, 0),
         (1, 0): (0, 1),
@@ -339,7 +336,7 @@
         (2, 1): (2, 1),
     }
     sends = {tile: ([(0, n)], [(1, n)]) for n, tile in enumerate(ALL)}
-    shared = (parts, half, other, lower, upper_inverse, sketch)
+    shared = (parts, half, other, turns(1), upper_inverse, sketch)
     ours = ((side_u, pieces[1], inner_u), (side_v, pieces[3], inner_v))
     u, v = compress(1, ALL, split, sends, (count, count), info, *ours, *shared)
     return u.reshape(tile_u.shape), v.reshape(tile_v.shape)

time: 124 us -> 116 us (0.935)
  the two profiles are of different devices: /device:TPU:104 before, /device:TPU:96 now
where the time goes in v1:
time: 116 us; the launch traced here: 115 us
  starting transfers between devices  41.3 us (36%)
  waiting for transfers between devices  36.6 us (32%)
  Pallas kernels  28.4 us (24%)
  other arithmetic  4.8 us (4%)
  local copies, waits for them, and re-layouts  1.84 us (2%)
    pallas_call x2, Pallas kernels, compress(): pl.pallas_call(functools.partial(compress_kernel, panel_id, tiles, places...  28.4 us
    ppermute x8, waiting for transfers between devices, along_z(): return lax.ppermute(part, ROW, pairs)  19.7 us
    ppermute x6, starting transfers between devices, spread_row(): lax.ppermute(part, 'y', [((k + s) % n_y, k) for k in range(n_y)])  11.2 us
    ppermute x8, starting transfers between devices, along_z(): return lax.ppermute(part, ROW, pairs)  8.74 us
    ppermute x6, waiting for transfers between devices, spread_row(): lax.ppermute(part, 'y', [((k + s) % n_y, k) for k in range(n_y)])  7.43 us
    ppermute x6, starting transfers between devices, spread_row(): lax.ppermute(pieces[k], ROW, [(root, k * n_z + root)])  6.15 us
    ppermute x2, starting transfers between devices, spread_col(): lax.ppermute(start, 'x', [(0, 3)])  5.63 us
    ppermute x2, waiting for transfers between devices, spread_col(): lax.ppermute(start, 'x', [(0, 3)])  4.93 us
  transfers between devices with their start and end apart: 32, of which 14 were waited for; matrix products, arithmetic and copies ran while one was open for 4% of the time, Pallas kernels for 0%

profile of v1, /device:TPU:96, one launch (start us, length us, event | category | flops | bytes accessed | tf_op | source)
XLA Modules:
  0.0 115.2 jit_solution(9976600571495243716)
XLA Ops:
  1.7 1.0 slice_select_fusion
  2.7 1.8 %collective-permute-start.10 = (bf16[3,512,128]{2,1,0:T(8,128)(2,1)S(1)}, bf16[3,512,128]{2,1,0:T(8,128)(2,1)S(1)}, u32[]{:S(2)}, u32[]{:S(2)}) collective-permute-start(bf16[3,512,128]{2,1,0:T(8,128)(2,1)S(1)} %slice_select_fusion), channel_id=1, source_target_pairs={{0,1},{8,9},{16,17},{24,25},{32,33},{40,41},{48,49},{56,57},{64,65... | collective-permute-start | bytes 1179656 | tf_op jit(solution)/shard_map/ppermute | solution.py:278
  7.8 3.6 %collective-permute-start.12 = (bf16[3,512,128]{2,1,0:T(8,128)(2,1)S(1)}, bf16[3,512,128]{2,1,0:T(8,128)(2,1)S(1)}, u32[]{:S(2)}, u32[]{:S(2)}) collective-permute-start(bf16[3,512,128]{2,1,0:T(8,128)(2,1)S(1)} %select_select_fusion.1), channel_id=1, source_target_pairs={{0,6},{1,7},{8,14},{9,15},{16,22},{17,23},{24,30},{25,31},{32,38},... | collective-permute-start | bytes 1179656 | tf_op jit(solution)/shard_map/ppermute | solution.py:280
  11.4 1.3 %collective-permute-start.11 = (bf16[3,512,128]{2,1,0:T(8,128)(2,1)S(1)}, bf16[3,512,128]{2,1,0:T(8,128)(2,1)S(1)}, u32[]{:S(2)}, u32[]{:S(2)}) collective-permute-start(bf16[3,512,128]{2,1,0:T(8,128)(2,1)S(1)} %select_select_fusion.1), channel_id=1, source_target_pairs={{0,2},{1,3},{8,10},{9,11},{16,18},{17,19},{24,26},{25,27},{32,34},... | collective-permute-start | bytes 1179656 | tf_op jit(solution)/shard_map/ppermute | solution.py:280
  13.5 1.3 %collective-permute-start.3 = (bf16[512,128]{1,0:T(8,128)(2,1)S(1)}, bf16[512,128]{1,0:T(8,128)(2,1)S(1)}, u32[]{:S(2)}, u32[]{:S(2)}) collective-permute-start(bf16[512,128]{1,0:T(8,128)(2,1)S(1)} %fusion.15), channel_id=1, source_target_pairs={{0,24},{64,88},{128,152},{192,216},{1,25},{65,89},{129,153},{193,2... | collective-permute-start | bytes 393224 | tf_op jit(solution)/shard_map/ppermute | solution.py:264
  14.8 4.9 %collective-permute-done.12 = bf16[3,512,128]{2,1,0:T(8,128)(2,1)S(1)} collective-permute-done((bf16[3,512,128]{2,1,0:T(8,128)(2,1)S(1)}, bf16[3,512,128]{2,1,0:T(8,128)(2,1)S(1)}, u32[]{:S(2)}, u32[]{:S(2)}) %collective-permute-start.12) | collective-permute-done | bytes 393248 | tf_op jit(solution)/shard_map/ppermute | solution.py:280
  19.7 1.3 %collective-permute-done.11 = bf16[3,512,128]{2,1,0:T(8,128)(2,1)S(1)} collective-permute-done((bf16[3,512,128]{2,1,0:T(8,128)(2,1)S(1)}, bf16[3,512,128]{2,1,0:T(8,128)(2,1)S(1)}, u32[]{:S(2)}, u32[]{:S(2)}) %collective-permute-start.11) | collective-permute-done | bytes 393248 | tf_op jit(solution)/shard_map/ppermute | solution.py:280
  22.6 2.2 %collective-permute-done.3 = bf16[512,128]{1,0:T(8,128)(2,1)S(1)} collective-permute-done((bf16[512,128]{1,0:T(8,128)(2,1)S(1)}, bf16[512,128]{1,0:T(8,128)(2,1)S(1)}, u32[]{:S(2)}, u32[]{:S(2)}) %collective-permute-start.3) | collective-permute-done | bytes 131104 | tf_op jit(solution)/shard_map/ppermute | solution.py:264
  24.9 1.3 %collective-permute-start.6 = (bf16[512,128]{1,0:T(8,128)(2,1)S(1)}, bf16[512,128]{1,0:T(8,128)(2,1)S(1)}, u32[]{:S(2)}, u32[]{:S(2)}) collective-permute-start(bf16[512,128]{1,0:T(8,128)(2,1)S(1)} %add_add_fusion.6), channel_id=1, source_target_pairs={{0,56},{24,16},{64,120},{88,80},{128,184},{152,144},{192,248},{216... | collective-permute-start | bytes 393224 | tf_op jit(solution)/shard_map/ppermute | solution.py:264
  26.2 2.2 %collective-permute-start.5 = (bf16[512,128]{1,0:T(8,128)(2,1)S(1)}, bf16[512,128]{1,0:T(8,128)(2,1)S(1)}, u32[]{:S(2)}, u32[]{:S(2)}) collective-permute-start(bf16[512,128]{1,0:T(8,128)(2,1)S(1)} %add_add_fusion.6), channel_id=1, source_target_pairs={{0,8},{24,32},{40,48},{64,72},{88,96},{104,112},{128,136},{152,160... | collective-permute-start | bytes 393224 | tf_op jit(solution)/shard_map/ppermute | solution.py:264
  28.7 2.2 %collective-permute-done.5 = bf16[512,128]{1,0:T(8,128)(2,1)S(1)} collective-permute-done((bf16[512,128]{1,0:T(8,128)(2,1)S(1)}, bf16[512,128]{1,0:T(8,128)(2,1)S(1)}, u32[]{:S(2)}, u32[]{:S(2)}) %collective-permute-start.5) | collective-permute-done | bytes 131104 | tf_op jit(solution)/shard_map/ppermute | solution.py:264
  30.9 1.7 %collective-permute-start.9 = (bf16[512,128]{1,0:T(8,128)(2,1)S(1)}, bf16[512,128]{1,0:T(8,128)(2,1)S(1)}, u32[]{:S(2)}, u32[]{:S(2)}) collective-permute-start(bf16[512,128]{1,0:T(8,128)(2,1)S(1)} %add_add_fusion.5.refs_2_), channel_id=1, source_target_pairs={{192,0},{0,64},{64,128},{128,192},{193,1},{1,65},{65,129},{129,193... | collective-permute-start | bytes 393224 | tf_op jit(solution)/shard_map/ppermute | solution.py:270
  32.6 2.9 %collective-permute-start.8 = (bf16[512,128]{1,0:T(8,128)(2,1)S(1)}, bf16[512,128]{1,0:T(8,128)(2,1)S(1)}, u32[]{:S(2)}, u32[]{:S(2)}) collective-permute-start(bf16[512,128]{1,0:T(8,128)(2,1)S(1)} %add_add_fusion.5.refs_2_), channel_id=1, source_target_pairs={{128,0},{192,64},{0,128},{64,192},{129,1},{193,65},{1,129},{65,193... | collective-permute-start | bytes 393224 | tf_op jit(solution)/shard_map/ppermute | solution.py:270
  35.5 1.3 %collective-permute-start.7 = (bf16[512,128]{1,0:T(8,128)(2,1)S(1)}, bf16[512,128]{1,0:T(8,128)(2,1)S(1)}, u32[]{:S(2)}, u32[]{:S(2)}) collective-permute-start(bf16[512,128]{1,0:T(8,128)(2,1)S(1)} %add_add_fusion.5.refs_2_), channel_id=1, source_target_pairs={{64,0},{128,64},{192,128},{0,192},{65,1},{129,65},{193,129},{1,193... | collective-permute-start | bytes 393224 | tf_op jit(solution)/shard_map/ppermute | solution.py:270
  37.4 1.1 collective-permute-done.9.refs_5_
  38.5 1.4 %collective-permute-done.8.refs_4_ = bf16[512,128]{1,0:T(8,128)(2,1)S(1)} collective-permute-done((bf16[512,128]{1,0:T(8,128)(2,1)S(1)}, bf16[512,128]{1,0:T(8,128)(2,1)S(1)}, u32[]{:S(2)}, u32[]{:S(2)}) %collective-permute-start.8) | collective-permute-done | bytes 131104 | tf_op jit(solution)/shard_map/ppermute | solution.py:270
  40.5 13.9 %shard_map.86 = (bf16[512,128]{1,0:T(8,128)(2,1)S(1)}, bf16[512,128]{1,0:T(8,128)(2,1)S(1)}, bf16[512,128]{1,0:T(8,128)(2,1)S(1)}, bf16[512,128]{1,0:T(8,128)(2,...) custom-call(s32[10]{0:T(128)S(1)} %concatenate.9.info, ...), custom_call_target="tpu_custom_call" | custom-call | flops 3019898880 | bytes 3145728 | tf_op jit(solution)/shard_map/pallas_call | solution.py:221
  55.1 1.3 %collective-permute-start.26 = (bf16[3,512,128]{2,1,0:T(8,128)(2,1)S(1)}, bf16[3,512,128]{2,1,0:T(8,128)(2,1)S(1)}, u32[]{:S(2)}, u32[]{:S(2)}) collective-permute-start(bf16[3,512,128]{2,1,0:T(8,128)(2,1)S(1)} %get-tuple-element.12.refs_0_), channel_id=1, source_target_pairs={{1,0},{9,8},{17,16},{25,24},{33,32},{41,40},{49,48},{57,56},{65,64... | collective-permute-start | bytes 1179656 | tf_op jit(solution)/shard_map/ppermute | solution.py:278
  56.4 2.3 %collective-permute-done.26 = bf16[3,512,128]{2,1,0:T(8,128)(2,1)S(1)} collective-permute-done((bf16[3,512,128]{2,1,0:T(8,128)(2,1)S(1)}, bf16[3,512,128]{2,1,0:T(8,128)(2,1)S(1)}, u32[]{:S(2)}, u32[]{:S(2)}) %collective-permute-start.26) | collective-permute-done | bytes 393248 | tf_op jit(solution)/shard_map/ppermute | solution.py:278
  58.8 2.0 %collective-permute-start.28 = (bf16[3,512,128]{2,1,0:T(8,128)(2,1)S(1)}, bf16[3,512,128]{2,1,0:T(8,128)(2,1)S(1)}, u32[]{:S(2)}, u32[]{:S(2)}) collective-permute-start(bf16[3,512,128]{2,1,0:T(8,128)(2,1)S(1)} %select_select_fusion), channel_id=1, source_target_pairs={{0,6},{1,7},{8,14},{9,15},{16,22},{17,23},{24,30},{25,31},{32,38},... | collective-permute-start | bytes 1179656 | tf_op jit(solution)/shard_map/ppermute | solution.py:280
  60.8 2.0 %collective-permute-start.27 = (bf16[3,512,128]{2,1,0:T(8,128)(2,1)S(1)}, bf16[3,512,128]{2,1,0:T(8,128)(2,1)}, u32[]{:S(2)}, u32[]{:S(2)}) collective-permute-start(bf16[3,512,128]{2,1,0:T(8,128)(2,1)S(1)} %select_select_fusion), channel_id=1, source_target_pairs={{0,2},{1,3},{8,10},{9,11},{16,18},{17,19},{24,26},{25,27},{32,34},... | collective-permute-start | bytes 1179656 | tf_op jit(solution)/shard_map/ppermute | solution.py:280
  62.8 1.5 %collective-permute-start.17 = (bf16[512,128]{1,0:T(8,128)(2,1)S(1)}, bf16[512,128]{1,0:T(8,128)(2,1)}, u32[]{:S(2)}, u32[]{:S(2)}) collective-permute-start(bf16[512,128]{1,0:T(8,128)(2,1)S(1)} %get-tuple-element.19), channel_id=1, source_target_pairs={{8,136},{9,137},{10,138},{11,139},{12,140},{13,141},{14,142},{15,1... | collective-permute-start | bytes 393224 | tf_op jit(solution)/shard_map/ppermute | solution.py:255
  64.4 1.3 %collective-permute-start.16 = (bf16[512,128]{1,0:T(8,128)(2,1)S(1)}, bf16[512,128]{1,0:T(8,128)(2,1)}, u32[]{:S(2)}, u32[]{:S(2)}) collective-permute-start(bf16[512,128]{1,0:T(8,128)(2,1)S(1)} %get-tuple-element.13.refs_1_), channel_id=1, source_target_pairs={{8,72},{9,73},{10,74},{11,75},{12,76},{13,77},{14,78},{15,79}} | collective-permute-start | bytes 393224 | tf_op jit(solution)/shard_map/ppermute | solution.py:255
  65.7 1.3 %collective-permute-start.18 = (bf16[512,128]{1,0:T(8,128)(2,1)S(1)}, bf16[512,128]{1,0:T(8,128)(2,1)}, u32[]{:S(2)}, u32[]{:S(2)}) collective-permute-start(bf16[512,128]{1,0:T(8,128)(2,1)S(1)} %get-tuple-element.16.refs_4_), channel_id=1, source_target_pairs={{8,200},{9,201},{10,202},{11,203},{12,204},{13,205},{14,206},{15,2... | collective-permute-start | bytes 393224 | tf_op jit(solution)/shard_map/ppermute | solution.py:255
  67.0 1.1 add_add_fusion.4
  70.3 1.1 add_add_fusion
  73.0 1.3 %collective-permute-start.22 = (bf16[512,128]{1,0:T(8,128)(2,1)S(1)}, bf16[512,128]{1,0:T(8,128)(2,1)S(1)}, u32[]{:S(2)}, u32[]{:S(2)}) collective-permute-start(bf16[512,128]{1,0:T(8,128)(2,1)S(1)} %add_add_fusion.3), channel_id=1, source_target_pairs={{8,0},{32,24},{72,64},{96,88},{136,128},{160,152},{200,192},{224,2... | collective-permute-start | bytes 393224 | tf_op jit(solution)/shard_map/ppermute | solution.py:264
  75.2 15.2 %collective-permute-done.22 = bf16[512,128]{1,0:T(8,128)(2,1)S(1)} collective-permute-done((bf16[512,128]{1,0:T(8,128)(2,1)S(1)}, bf16[512,128]{1,0:T(8,128)(2,1)S(1)}, u32[]{:S(2)}, u32[]{:S(2)}) %collective-permute-start.22) | collective-permute-done | bytes 131104 | tf_op jit(solution)/shard_map/ppermute | solution.py:264
  90.4 1.6 %collective-permute-start.25 = (bf16[512,128]{1,0:T(8,128)(2,1)S(1)}, bf16[512,128]{1,0:T(8,128)(2,1)S(1)}, u32[]{:S(2)}, u32[]{:S(2)}) collective-permute-start(bf16[512,128]{1,0:T(8,128)(2,1)S(1)} %add_add_fusion.2.refs_6_), channel_id=1, source_target_pairs={{192,0},{0,64},{64,128},{128,192},{193,1},{1,65},{65,129},{129,193... | collective-permute-start | bytes 393224 | tf_op jit(solution)/shard_map/ppermute | solution.py:270
  92.0 3.7 %collective-permute-start.24 = (bf16[512,128]{1,0:T(8,128)(2,1)S(1)}, bf16[512,128]{1,0:T(8,128)(2,1)S(1)}, u32[]{:S(2)}, u32[]{:S(2)}) collective-permute-start(bf16[512,128]{1,0:T(8,128)(2,1)S(1)} %add_add_fusion.2.refs_6_), channel_id=1, source_target_pairs={{128,0},{192,64},{0,128},{64,192},{129,1},{193,65},{1,129},{65,193... | collective-permute-start | bytes 393224 | tf_op jit(solution)/shard_map/ppermute | solution.py:270
  97.2 2.9 %collective-permute-done.24.refs_8_ = bf16[512,128]{1,0:T(8,128)(2,1)S(1)} collective-permute-done((bf16[512,128]{1,0:T(8,128)(2,1)S(1)}, bf16[512,128]{1,0:T(8,128)(2,1)S(1)}, u32[]{:S(2)}, u32[]{:S(2)}) %collective-permute-start.24) | collective-permute-done | bytes 131104 | tf_op jit(solution)/shard_map/ppermute | solution.py:270
  100.7 14.5 %shard_map.87 = (bf16[6,512,128]{2,1,0:T(8,128)(2,1)}, bf16[6,512,128]{2,1,0:T(8,128)(2,1)}) custom-call(s32[10]{0:T(128)S(1)} %concatenate.9.info, bf16[3,512,128]{2,1,0:T(8,128)(2,1)S(1)} %get-tuple-element.12.refs_0_, bf16[512,128]{1,0:T(8,128)(2,1)S(1)} %get-tuple-element.13.refs_1_, bf16[2,512,128]{2,1,0:T(8,128)(2,1)S(1)} %get-tuple-element.14.refs_2_, ...), custom_call_target="tpu_custom_call" | custom-call | flops 3019898880 | bytes 3145728 | tf_op jit(solution)/shard_map/pallas_call | solution.py:221
  (78 shorter events, 15.5 us)
Async XLA Ops:
  2.7 5.0 %collective-permute-start.10 = (bf16[3,512,128]{2,1,0:T(8,128)(2,1)S(1)}, bf16[3,512,128]{2,1,0:T(8,128)(2,1)S(1)}, u32[]{:S(2)}, u32[]{:S(2)}) collective-permute-start(bf16[3,512,128]{2,1,0:T(8,128)(2,1)S(1)} %slice_select_fusion), channel_id=1, source_target_pairs={{0,1},{8,9},{16,17},{24,25},{32,33},{40,41},{48,49},{56,57},{64,65... | collective-permute-start | bytes 1179656 | tf_op jit(solution)/shard_map/ppermute | solution.py:278
  5.6 7.2 %collective-permute-start.1 = (bf16[512,128]{1,0:T(8,128)(2,1)S(1)}, bf16[512,128]{1,0:T(8,128)(2,1)S(1)}, u32[]{:S(2)}, u32[]{:S(2)}) collective-permute-start(bf16[512,128]{1,0:T(8,128)(2,1)S(1)} %get-tuple-element.26), channel_id=1, source_target_pairs={{0,128},{1,129},{2,130},{3,131},{4,132},{5,133},{6,134},{7,135}} | collective-permute-start | bytes 393224 | tf_op jit(solution)/shard_map/ppermute | solution.py:255
  6.2 6.5 %collective-permute-start.2 = (bf16[512,128]{1,0:T(8,128)(2,1)S(1)}, bf16[512,128]{1,0:T(8,128)(2,1)S(1)}, u32[]{:S(2)}, u32[]{:S(2)}) collective-permute-start(bf16[512,128]{1,0:T(8,128)(2,1)S(1)} %get-tuple-element.27), channel_id=1, source_target_pairs={{0,192},{1,193},{2,194},{3,195},{4,196},{5,197},{6,198},{7,199}} | collective-permute-start | bytes 393224 | tf_op jit(solution)/shard_map/ppermute | solution.py:255
  6.9 5.8 %collective-permute-start = (bf16[512,128]{1,0:T(8,128)(2,1)S(1)}, bf16[512,128]{1,0:T(8,128)(2,1)S(1)}, u32[]{:S(2)}, u32[]{:S(2)}) collective-permute-start(bf16[512,128]{1,0:T(8,128)(2,1)S(1)} %get-tuple-element.36), channel_id=1, source_target_pairs={{0,64},{1,65},{2,66},{3,67},{4,68},{5,69},{6,70},{7,71}} | collective-permute-start | bytes 393224 | tf_op jit(solution)/shard_map/ppermute | solution.py:255
  7.8 11.9 %collective-permute-start.12 = (bf16[3,512,128]{2,1,0:T(8,128)(2,1)S(1)}, bf16[3,512,128]{2,1,0:T(8,128)(2,1)S(1)}, u32[]{:S(2)}, u32[]{:S(2)}) collective-permute-start(bf16[3,512,128]{2,1,0:T(8,128)(2,1)S(1)} %select_select_fusion.1), channel_id=1, source_target_pairs={{0,6},{1,7},{8,14},{9,15},{16,22},{17,23},{24,30},{25,31},{32,38},... | collective-permute-start | bytes 1179656 | tf_op jit(solution)/shard_map/ppermute | solution.py:280
  11.4 9.7 %collective-permute-start.11 = (bf16[3,512,128]{2,1,0:T(8,128)(2,1)S(1)}, bf16[3,512,128]{2,1,0:T(8,128)(2,1)S(1)}, u32[]{:S(2)}, u32[]{:S(2)}) collective-permute-start(bf16[3,512,128]{2,1,0:T(8,128)(2,1)S(1)} %select_select_fusion.1), channel_id=1, source_target_pairs={{0,2},{1,3},{8,10},{9,11},{16,18},{17,19},{24,26},{25,27},{32,34},... | collective-permute-start | bytes 1179656 | tf_op jit(solution)/shard_map/ppermute | solution.py:280
  12.8 9.8 %collective-permute-start.4 = (bf16[512,128]{1,0:T(8,128)(2,1)S(1)}, bf16[512,128]{1,0:T(8,128)(2,1)S(1)}, u32[]{:S(2)}, u32[]{:S(2)}) collective-permute-start(bf16[512,128]{1,0:T(8,128)(2,1)S(1)} %fusion.15), channel_id=1, source_target_pairs={{0,40},{64,104},{128,168},{192,232},{1,41},{65,105},{129,169},{193... | collective-permute-start | bytes 393224 | tf_op jit(solution)/shard_map/ppermute | solution.py:264
  13.5 11.4 %collective-permute-start.3 = (bf16[512,128]{1,0:T(8,128)(2,1)S(1)}, bf16[512,128]{1,0:T(8,128)(2,1)S(1)}, u32[]{:S(2)}, u32[]{:S(2)}) collective-permute-start(bf16[512,128]{1,0:T(8,128)(2,1)S(1)} %fusion.15), channel_id=1, source_target_pairs={{0,24},{64,88},{128,152},{192,216},{1,25},{65,89},{129,153},{193,2... | collective-permute-start | bytes 393224 | tf_op jit(solution)/shard_map/ppermute | solution.py:264
  21.1 7.3 %collective-permute-start.13 = (bf16[3,256,128]{2,1,0:T(8,128)(2,1)S(1)}, bf16[3,256,128]{2,1,0:T(8,128)(2,1)S(1)}, u32[]{:S(2)}, u32[]{:S(2)}) collective-permute-start(bf16[3,256,128]{2,1,0:T(8,128)(2,1)S(1)} %get-tuple-element.30), channel_id=1, source_target_pairs={{2,4},{3,5},{10,12},{11,13},{18,20},{19,21},{26,28},{27,29},{34,36... | collective-permute-start | bytes 589832 | tf_op jit(solution)/shard_map/ppermute | solution.py:283
  21.8 6.6 %collective-permute-start.14 = (bf16[3,256,128]{2,1,0:T(8,128)(2,1)S(1)}, bf16[3,256,128]{2,1,0:T(8,128)(2,1)S(1)}, u32[]{:S(2)}, u32[]{:S(2)}) collective-permute-start(bf16[3,256,128]{2,1,0:T(8,128)(2,1)S(1)} %get-tuple-element.31), channel_id=1, source_target_pairs={{6,4},{7,5},{14,12},{15,13},{22,20},{23,21},{30,28},{31,29},{38,36... | collective-permute-start | bytes 589832 | tf_op jit(solution)/shard_map/ppermute | solution.py:284
  24.9 3.8 %collective-permute-start.6 = (bf16[512,128]{1,0:T(8,128)(2,1)S(1)}, bf16[512,128]{1,0:T(8,128)(2,1)S(1)}, u32[]{:S(2)}, u32[]{:S(2)}) collective-permute-start(bf16[512,128]{1,0:T(8,128)(2,1)S(1)} %add_add_fusion.6), channel_id=1, source_target_pairs={{0,56},{24,16},{64,120},{88,80},{128,184},{152,144},{192,248},{216... | collective-permute-start | bytes 393224 | tf_op jit(solution)/shard_map/ppermute | solution.py:264
  26.2 4.7 %collective-permute-start.5 = (bf16[512,128]{1,0:T(8,128)(2,1)S(1)}, bf16[512,128]{1,0:T(8,128)(2,1)S(1)}, u32[]{:S(2)}, u32[]{:S(2)}) collective-permute-start(bf16[512,128]{1,0:T(8,128)(2,1)S(1)} %add_add_fusion.6), channel_id=1, source_target_pairs={{0,8},{24,32},{40,48},{64,72},{88,96},{104,112},{128,136},{152,160... | collective-permute-start | bytes 393224 | tf_op jit(solution)/shard_map/ppermute | solution.py:264
  28.6 11.9 %collective-permute-start.15 = (bf16[3,512,128]{2,1,0:T(8,128)(2,1)S(1)}, bf16[3,512,128]{2,1,0:T(8,128)(2,1)S(1)}, u32[]{:S(2)}, u32[]{:S(2)}) collective-permute-start(bf16[3,512,128]{2,1,0:T(8,128)(2,1)S(1)} %maximum_add_fusion.refs_6_), channel_id=1, source_target_pairs={{0,1},{1,0},{2,3},{3,2},{4,5},{5,4},{6,7},{7,6},{8,9},{9,8},{10,11... | collective-permute-start | bytes 1179656 | tf_op jit(solution)/shard_map/ppermute | solution.py:286
  30.9 7.6 %collective-permute-start.9 = (bf16[512,128]{1,0:T(8,128)(2,1)S(1)}, bf16[512,128]{1,0:T(8,128)(2,1)S(1)}, u32[]{:S(2)}, u32[]{:S(2)}) collective-permute-start(bf16[512,128]{1,0:T(8,128)(2,1)S(1)} %add_add_fusion.5.refs_2_), channel_id=1, source_target_pairs={{192,0},{0,64},{64,128},{128,192},{193,1},{1,65},{65,129},{129,193... | collective-permute-start | bytes 393224 | tf_op jit(solution)/shard_map/ppermute | solution.py:270
  32.6 7.3 %collective-permute-start.8 = (bf16[512,128]{1,0:T(8,128)(2,1)S(1)}, bf16[512,128]{1,0:T(8,128)(2,1)S(1)}, u32[]{:S(2)}, u32[]{:S(2)}) collective-permute-start(bf16[512,128]{1,0:T(8,128)(2,1)S(1)} %add_add_fusion.5.refs_2_), channel_id=1, source_target_pairs={{128,0},{192,64},{0,128},{64,192},{129,1},{193,65},{1,129},{65,193... | collective-permute-start | bytes 393224 | tf_op jit(solution)/shard_map/ppermute | solution.py:270
  35.5 5.0 %collective-permute-start.7 = (bf16[512,128]{1,0:T(8,128)(2,1)S(1)}, bf16[512,128]{1,0:T(8,128)(2,1)S(1)}, u32[]{:S(2)}, u32[]{:S(2)}) collective-permute-start(bf16[512,128]{1,0:T(8,128)(2,1)S(1)} %add_add_fusion.5.refs_2_), channel_id=1, source_target_pairs={{64,0},{128,64},{192,128},{0,192},{65,1},{129,65},{193,129},{1,193... | collective-permute-start | bytes 393224 | tf_op jit(solution)/shard_map/ppermute | solution.py:270
  55.1 3.6 %collective-permute-start.26 = (bf16[3,512,128]{2,1,0:T(8,128)(2,1)S(1)}, bf16[3,512,128]{2,1,0:T(8,128)(2,1)S(1)}, u32[]{:S(2)}, u32[]{:S(2)}) collective-permute-start(bf16[3,512,128]{2,1,0:T(8,128)(2,1)S(1)} %get-tuple-element.12.refs_0_), channel_id=1, source_target_pairs={{1,0},{9,8},{17,16},{25,24},{33,32},{41,40},{49,48},{57,56},{65,64... | collective-permute-start | bytes 1179656 | tf_op jit(solution)/shard_map/ppermute | solution.py:278
  58.8 10.7 %collective-permute-start.28 = (bf16[3,512,128]{2,1,0:T(8,128)(2,1)S(1)}, bf16[3,512,128]{2,1,0:T(8,128)(2,1)S(1)}, u32[]{:S(2)}, u32[]{:S(2)}) collective-permute-start(bf16[3,512,128]{2,1,0:T(8,128)(2,1)S(1)} %select_select_fusion), channel_id=1, source_target_pairs={{0,6},{1,7},{8,14},{9,15},{16,22},{17,23},{24,30},{25,31},{32,38},... | collective-permute-start | bytes 1179656 | tf_op jit(solution)/shard_map/ppermute | solution.py:280
  60.8 9.5 %collective-permute-start.27 = (bf16[3,512,128]{2,1,0:T(8,128)(2,1)S(1)}, bf16[3,512,128]{2,1,0:T(8,128)(2,1)}, u32[]{:S(2)}, u32[]{:S(2)}) collective-permute-start(bf16[3,512,128]{2,1,0:T(8,128)(2,1)S(1)} %select_select_fusion), channel_id=1, source_target_pairs={{0,2},{1,3},{8,10},{9,11},{16,18},{17,19},{24,26},{25,27},{32,34},... | collective-permute-start | bytes 1179656 | tf_op jit(solution)/shard_map/ppermute | solution.py:280
  62.8 4.1 %collective-permute-start.17 = (bf16[512,128]{1,0:T(8,128)(2,1)S(1)}, bf16[512,128]{1,0:T(8,128)(2,1)}, u32[]{:S(2)}, u32[]{:S(2)}) collective-permute-start(bf16[512,128]{1,0:T(8,128)(2,1)S(1)} %get-tuple-element.19), channel_id=1, source_target_pairs={{8,136},{9,137},{10,138},{11,139},{12,140},{13,141},{14,142},{15,1... | collective-permute-start | bytes 393224 | tf_op jit(solution)/shard_map/ppermute | solution.py:255
  64.4 2.6 %collective-permute-start.16 = (bf16[512,128]{1,0:T(8,128)(2,1)S(1)}, bf16[512,128]{1,0:T(8,128)(2,1)}, u32[]{:S(2)}, u32[]{:S(2)}) collective-permute-start(bf16[512,128]{1,0:T(8,128)(2,1)S(1)} %get-tuple-element.13.refs_1_), channel_id=1, source_target_pairs={{8,72},{9,73},{10,74},{11,75},{12,76},{13,77},{14,78},{15,79}} | collective-permute-start | bytes 393224 | tf_op jit(solution)/shard_map/ppermute | solution.py:255
  65.7 1.3 %collective-permute-start.18 = (bf16[512,128]{1,0:T(8,128)(2,1)S(1)}, bf16[512,128]{1,0:T(8,128)(2,1)}, u32[]{:S(2)}, u32[]{:S(2)}) collective-permute-start(bf16[512,128]{1,0:T(8,128)(2,1)S(1)} %get-tuple-element.16.refs_4_), channel_id=1, source_target_pairs={{8,200},{9,201},{10,202},{11,203},{12,204},{13,205},{14,206},{15,2... | collective-permute-start | bytes 393224 | tf_op jit(solution)/shard_map/ppermute | solution.py:255
  68.1 4.9 %collective-permute-start.20 = (bf16[512,128]{1,0:T(8,128)(2,1)S(1)}, bf16[512,128]{1,0:T(8,128)(2,1)S(1)}, u32[]{:S(2)}, u32[]{:S(2)}) collective-permute-start(bf16[512,128]{1,0:T(8,128)(2,1)S(1)} %add_add_fusion.4), channel_id=1, source_target_pairs={{8,48},{72,112},{136,176},{200,240},{9,49},{73,113},{137,177},{201... | collective-permute-start | bytes 393224 | tf_op jit(solution)/shard_map/ppermute | solution.py:264
  68.7 4.2 %collective-permute-start.19 = (bf16[512,128]{1,0:T(8,128)(2,1)S(1)}, bf16[512,128]{1,0:T(8,128)(2,1)S(1)}, u32[]{:S(2)}, u32[]{:S(2)}) collective-permute-start(bf16[512,128]{1,0:T(8,128)(2,1)S(1)} %add_add_fusion.4), channel_id=1, source_target_pairs={{8,32},{72,96},{136,160},{200,224},{9,33},{73,97},{137,161},{201,2... | collective-permute-start | bytes 393224 | tf_op jit(solution)/shard_map/ppermute | solution.py:264
  71.4 3.5 %collective-permute-start.29 = (bf16[3,256,128]{2,1,0:T(8,128)(2,1)S(1)}, bf16[3,256,128]{2,1,0:T(8,128)(2,1)S(1)}, u32[]{:S(2)}, u32[]{:S(2)}) collective-permute-start(bf16[3,256,128]{2,1,0:T(8,128)(2,1)S(1)} %get-tuple-element.28), channel_id=1, source_target_pairs={{2,4},{3,5},{10,12},{11,13},{18,20},{19,21},{26,28},{27,29},{34,36... | collective-permute-start | bytes 589832 | tf_op jit(solution)/shard_map/ppermute | solution.py:283
  72.1 2.9 %collective-permute-start.30 = (bf16[3,256,128]{2,1,0:T(8,128)(2,1)S(1)}, bf16[3,256,128]{2,1,0:T(8,128)(2,1)S(1)}, u32[]{:S(2)}, u32[]{:S(2)}) collective-permute-start(bf16[3,256,128]{2,1,0:T(8,128)(2,1)S(1)} %get-tuple-element.29), channel_id=1, source_target_pairs={{6,4},{7,5},{14,12},{15,13},{22,20},{23,21},{30,28},{31,29},{38,36... | collective-permute-start | bytes 589832 | tf_op jit(solution)/shard_map/ppermute | solution.py:284
  73.0 17.4 %collective-permute-start.22 = (bf16[512,128]{1,0:T(8,128)(2,1)S(1)}, bf16[512,128]{1,0:T(8,128)(2,1)S(1)}, u32[]{:S(2)}, u32[]{:S(2)}) collective-permute-start(bf16[512,128]{1,0:T(8,128)(2,1)S(1)} %add_add_fusion.3), channel_id=1, source_target_pairs={{8,0},{32,24},{72,64},{96,88},{136,128},{160,152},{200,192},{224,2... | collective-permute-start | bytes 393224 | tf_op jit(solution)/shard_map/ppermute | solution.py:264
  74.3 16.1 %collective-permute-start.21 = (bf16[512,128]{1,0:T(8,128)(2,1)S(1)}, bf16[512,128]{1,0:T(8,128)(2,1)S(1)}, u32[]{:S(2)}, u32[]{:S(2)}) collective-permute-start(bf16[512,128]{1,0:T(8,128)(2,1)S(1)} %add_add_fusion.3), channel_id=1, source_target_pairs={{8,16},{32,40},{48,56},{72,80},{96,104},{112,120},{136,144},{160,1... | collective-permute-start | bytes 393224 | tf_op jit(solution)/shard_map/ppermute | solution.py:264
  75.1 25.6 %collective-permute-start.31 = (bf16[3,512,128]{2,1,0:T(8,128)(2,1)S(1)}, bf16[3,512,128]{2,1,0:T(8,128)(2,1)S(1)}, u32[]{:S(2)}, u32[]{:S(2)}) collective-permute-start(bf16[3,512,128]{2,1,0:T(8,128)(2,1)S(1)} %maximum_add_fusion.1.refs_10_), channel_id=1, source_target_pairs={{0,1},{1,0},{2,3},{3,2},{4,5},{5,4},{6,7},{7,6},{8,9},{9,8},{10,11... | collective-permute-start | bytes 1179656 | tf_op jit(solution)/shard_map/ppermute | solution.py:286
  90.4 6.8 %collective-permute-start.25 = (bf16[512,128]{1,0:T(8,128)(2,1)S(1)}, bf16[512,128]{1,0:T(8,128)(2,1)S(1)}, u32[]{:S(2)}, u32[]{:S(2)}) collective-permute-start(bf16[512,128]{1,0:T(8,128)(2,1)S(1)} %add_add_fusion.2.refs_6_), channel_id=1, source_target_pairs={{192,0},{0,64},{64,128},{128,192},{193,1},{1,65},{65,129},{129,193... | collective-permute-start | bytes 393224 | tf_op jit(solution)/shard_map/ppermute | solution.py:270
  92.0 8.1 %collective-permute-start.24 = (bf16[512,128]{1,0:T(8,128)(2,1)S(1)}, bf16[512,128]{1,0:T(8,128)(2,1)S(1)}, u32[]{:S(2)}, u32[]{:S(2)}) collective-permute-start(bf16[512,128]{1,0:T(8,128)(2,1)S(1)} %add_add_fusion.2.refs_6_), channel_id=1, source_target_pairs={{128,0},{192,64},{0,128},{64,192},{129,1},{193,65},{1,129},{65,193... | collective-permute-start | bytes 393224 | tf_op jit(solution)/shard_map/ppermute | solution.py:270
  95.7 5.0 %collective-permute-start.23 = (bf16[512,128]{1,0:T(8,128)(2,1)S(1)}, bf16[512,128]{1,0:T(8,128)(2,1)S(1)}, u32[]{:S(2)}, u32[]{:S(2)}) collective-permute-start(bf16[512,128]{1,0:T(8,128)(2,1)S(1)} %add_add_fusion.2.refs_6_), channel_id=1, source_target_pairs={{64,0},{128,64},{192,128},{0,192},{65,1},{129,65},{193,129},{1,193... | collective-permute-start | bytes 393224 | tf_op jit(solution)/shard_map/ppermute | solution.py:270
  (9 other events, 72.4 us)
